TPU v7x, 512 devices: a whole 4x8x8 slice. The times are simulated.
512 devices in a mesh: dp: 8 (over y), slab: 16 (over x_hi, z), view: 4 (over x_lo, core).
Axes of the slice: x: 4 (x_hi: 2, x_lo: 2; x = x_hi * 2 + x_lo), y: 8, z: 8, core: 2. Of those that a mesh axis runs over, the one named last changes fastest.
Arguments:
- latent_feats: bfloat16 [8, 4, 64, 32, 256], P('dp', 'view', 'slab'), may hold values from -6 to 6
- conv_weight: bfloat16 [2304, 256], P(('dp', 'slab')), may hold values from -0.125 to 0.125
- kv_weight: bfloat16 [256, 1536], P(('dp', 'slab')), may hold values from -0.375 to 0.375
- stream: bfloat16 [8, 4, 64, 32, 768], P('dp', 'view', 'slab'), may hold values from -6 to 6
- queries: bfloat16 [8, 4, 64, 32, 768], P('dp', 'view', 'slab'), may hold values from -102 to 102
- norm_gain: float32 [768], replicated, may hold values from 0.1 to 1.9
- up_weight: bfloat16 [768, 3072], P(('dp', 'slab'), 'view'), may hold values from -0.21875 to 0.21875
- down_weight: bfloat16 [768, 3072], P(('dp', 'slab'), 'view'), may hold values from -0.109375 to 0.109375
- band_start: int32 [8, 4, 64, 4], P('dp', 'view', 'slab'), may hold values from 0 to 63, as said below
- band_end: int32 [8, 4, 64, 4], P('dp', 'view', 'slab'), may hold values from 1 to 64
- visibility: int32 [8, 4, 4], P('dp'), may hold values 0 or 1
Outputs:
- output: bfloat16 [8, 4, 64, 32, 768], P('dp', 'view', 'slab')
Inputs may be any that keep to these rules, and one draw needn't show every extreme that they name: band_end - band_start lies in 1 to 4 and equals 4 for some rows in every draw; for a row r both bounds lie within rows (r // 4) * 4 - 1 to (r // 4 + 1) * 4 + 1, clipped to the grid.
All inputs are finite; a program needn't handle non-finite values. No bound on the sum of `visibility` on one device may be relied on, other than what follows from the above.
Results may differ from a plain program's by a relative error of at most 0.0085.
Values may be sent and summed in bfloat16 or wider, within the bound.
No kernel may reach another device: no remote copies, remote signals or barrier semaphores. Data moves between devices by JAX's collectives and lax.ppermute only.
A program may use at most 64 MiB of HBM per device.

v0:
```python
import jax
import jax.numpy as jnp
import numpy as np
from jax import lax
from jax.experimental import pallas as pl
from jax.experimental.pallas import tpu as pltpu
from jax.sharding import Mesh
from jax.sharding import PartitionSpec as P

HEAD_DIM = 64
SLAB = ("slab_0", "slab_1")
DP_SLAB = ("dp", "slab_0", "slab_1")
BF = jnp.bfloat16
F32 = jnp.float32

VMEM = pl.BlockSpec(memory_space=pltpu.VMEM)
HBM = pl.BlockSpec(memory_space=pltpu.HBM)
SMEM = pl.BlockSpec(memory_space=pltpu.SMEM)


def one_hot(size, rows):
    place = lax.broadcasted_iota(jnp.int32, (1, size), 1)
    z = place // (16 * rows)
    rest = place % (16 * rows)
    row = (rest // rows * 8 + z) * rows + rest % rows
    here = lax.broadcasted_iota(jnp.int32, (size, size), 0)
    return jnp.where(here == row, 1.0, 0.0).astype(BF)


def conv_kernel(where_ref, rows_ref, own_ref, other_ref, out_ref, x_ref, sem):
    copy = pltpu.make_async_copy(rows_ref, x_ref, sem)
    copy.start()
    copy.wait()
    lower = (where_ref[2] >> 1) == 0
    shifted, feats = [], []
    for k in range(2):
        rows = x_ref[k * 256 : (k + 1) * 256, :]
        x = rows.astype(F32)
        col = lax.broadcasted_iota(jnp.int32, x.shape, 0) % 32
        left = jnp.where(col == 0, 0.0, pltpu.roll(x, 1, 0)).astype(BF)
        right = jnp.where(col == 31, 0.0, pltpu.roll(x, x.shape[0] - 1, 0)).astype(BF)
        shifted.append((left, rows, right))
        feats.append(jnp.where(lower, x[32:224, :128], x[32:224, 128:]))
    feats = jnp.concatenate(feats, axis=0)

    def tap_weight(ref, tap):
        at, end, pieces = tap * 256, (tap + 1) * 256, []
        while at < end:
            d, low = divmod(at, 288)
            high = min(288, low + end - at)
            pieces.append(ref[d, low:high, :])
            at += high - low
        return pieces[0] if len(pieces) == 1 else jnp.concatenate(pieces, axis=0)

    for core, ref in ((0, own_ref), (1, other_ref)):

        @pl.when(where_ref[0] == core)
        def _(ref=ref):
            conv = jnp.zeros((384, 128), F32)
            for tap in range(9):
                at = slice(tap // 3 * 32, tap // 3 * 32 + 192)
                rows = jnp.concatenate([views[tap % 3][at] for views in shifted], axis=0)
                conv = conv + jnp.dot(rows, tap_weight(ref, tap), preferred_element_type=F32)
            silu = conv / (1.0 + jnp.exp(-conv))
            out_ref[...] = (feats + silu).astype(BF)


def attention_kernel(
    where_ref,
    start_ref,
    end_ref,
    seen_ref,
    enc_ref,
    own_ref,
    other_ref,
    q_ref,
    stream_ref,
    gain_ref,
    normed_ref,
    far_ref,
    kv_ref,
    bias_ref,
    residual_ref,
    sems,
):
    first = where_ref[0] == 0
    first_row = where_ref[1]
    enc = []
    for view in range(4):
        tiles = []
        for tile in range(2):
            device = tile * 2 + view % 2
            at = device * 384 + (0 if device == view else 192)
            tiles.append(enc_ref[at : at + 192, :])
        enc.append(jnp.concatenate(tiles, axis=1))
    enc = jnp.concatenate(enc, axis=0)
    enc = jnp.dot(enc, one_hot(256, 2), preferred_element_type=F32).astype(BF)
    for couple in range(6):
        tiles = []
        for tile in (2 * couple, 2 * couple + 1):
            at = slice(tile * 32, (tile + 1) * 32)
            tiles.append(
                jnp.concatenate(
                    [jnp.where(first, other_ref[z, at, :], own_ref[z, at, :]) for z in range(8)],
                    axis=0,
                )
            )
        weight = jnp.concatenate(tiles, axis=1)
        kv = jnp.dot(enc, weight, preferred_element_type=F32).astype(BF)
        kv_ref[2 * couple] = kv[:, :128]
        kv_ref[2 * couple + 1] = kv[:, 128:]
    lane = lax.broadcasted_iota(jnp.int32, (1, 768), 1)
    key_view = lane // 192
    key_row = first_row - 1 + (lane % 192) // 32
    for r in range(4):
        low = jnp.zeros((1, 768), jnp.int32)
        high = jnp.zeros((1, 768), jnp.int32)
        for u in range(4):
            mine = key_view == u
            low = jnp.where(mine, start_ref[r, u], low)
            high = jnp.where(mine, jnp.where(seen_ref[u] == 1, end_ref[r, u], -1), high)
        bias = jnp.where((low <= key_row) & (key_row < high), 0.0, -1e30)
        bias_ref[r * 32 : (r + 1) * 32, :] = jnp.broadcast_to(bias, (32, 768))
    left = lax.broadcasted_iota(jnp.int32, (128, 128), 1) < HEAD_DIM
    square = jnp.zeros((128, 1), F32)
    copies = []
    for pair in range(6):
        q = q_ref[:, pair * 128 : (pair + 1) * 128]
        zero = jnp.zeros_like(q)
        keys = kv_ref[pair]
        values = kv_ref[6 + pair]
        both = jnp.concatenate([jnp.where(left, q, zero), jnp.where(left, zero, q)], axis=0)
        scores = lax.dot_general(
            both, keys, (((1,), (1,)), ((), ())), preferred_element_type=F32
        )
        bias = bias_ref[...]
        scores = scores * HEAD_DIM ** (-0.5) + jnp.concatenate([bias, bias], axis=0)
        weights = jnp.exp(scores - jnp.max(scores, axis=-1, keepdims=True))
        share = 1.0 / jnp.sum(weights, axis=-1, keepdims=True)
        outs = jnp.dot(weights.astype(BF), values, preferred_element_type=F32) * share
        attended = jnp.where(left, outs[:128], outs[128:])
        cols = slice(pair * 128, (pair + 1) * 128)
        residual = stream_ref[:, cols].astype(F32) + attended
        residual_ref[:, cols] = residual
        copies.append(
            pltpu.make_async_copy(residual_ref.at[:, cols], far_ref.at[:, cols], sems.at[pair])
        )
        copies[-1].start()
        square = square + jnp.sum(residual * residual, axis=-1, keepdims=True)
    scale = lax.rsqrt(square * (1.0 / 768) + 1e-6)
    normed_ref[...] = (residual_ref[...] * scale * gain_ref[...]).astype(BF)
    for copy in copies:
        copy.wait()


def gelu(v):
    return 0.5 * v * (1.0 + jnp.tanh(0.7978845608028654 * (v + 0.044715 * (v * v * v))))


def blocks_of(where_ref, tok_ref, w_ref, out_refs, chip_flip, flips):
    blocks = []
    for flip in flips:
        view = where_ref[2] ^ (chip_flip * 2 + flip)
        blocks.append(tok_ref[pl.ds(pl.multiple_of(view * 128, 128), 128), :])

    def gathered(at):
        tiles = []
        for tile in range(6):
            rows = slice(at + tile * 96, at + (tile + 1) * 96)
            tiles.append(jnp.concatenate([w_ref[d, rows, :] for d in range(8)], axis=0))
        return jnp.concatenate(tiles, axis=1)

    tokens = jnp.concatenate(blocks, axis=0)
    hidden = gelu(jnp.dot(tokens, gathered(0), preferred_element_type=F32)).astype(BF)
    parts = last_dims(hidden, gathered(576)).astype(BF)
    for k, out_ref in enumerate(out_refs):
        out_ref[...] = parts[k * 128 : (k + 1) * 128]


def cross_kernel(where_ref, tok_ref, w_ref, cross_ref):
    blocks_of(where_ref, tok_ref, w_ref, (cross_ref,), 1, (1,))


def same_kernel(where_ref, tok_ref, w_ref, same_ref):
    blocks_of(where_ref, tok_ref, w_ref, (same_ref,), 1, (0,))


def near_kernel(where_ref, tok_ref, w_ref, own_ref, sibling_ref, swap_ref):
    blocks_of(where_ref, tok_ref, w_ref, (own_ref, sibling_ref), 0, (0, 1))
    swap_ref[...] = one_hot(768, 6)


def swap_kernel(where_ref, tok_ref, out_ref):
    @pl.when(where_ref[0] == 0)
    def _():
        out_ref[...] = tok_ref[...]

    @pl.when(where_ref[0] != 0)
    def _():
        out_ref[...] = jnp.dot(tok_ref[...], one_hot(768, 6), preferred_element_type=F32).astype(BF)


def sum_kernel(
    where_ref, own_ref, sibling_ref, same_ref, cross_ref, swap_ref, residual_ref, out_ref
):
    alike = own_ref[...].astype(F32) + same_ref[...].astype(F32)
    unlike = sibling_ref[...].astype(F32) + cross_ref[...].astype(F32)
    first = where_ref[0] == 0
    odd = jnp.where(first, unlike, alike)
    even = jnp.where(first, alike, unlike)
    high = odd.astype(BF)
    low = (odd - high.astype(F32)).astype(BF)
    both = last_dims(jnp.concatenate([high, low], axis=0), swap_ref[...])
    odd = both[:128] + both[128:]
    out_ref[...] = (residual_ref[...] + (even + odd)).astype(BF)


def last_dims(a, b):
    return lax.dot_general(a, b, (((1,), (1,)), ((), ())), preferred_element_type=F32)


def pack_kernel(where_ref, *refs):
    (sources, out_ref, held, sems) = (refs[:4], refs[4], refs[5:9], refs[9])
    copies = [pltpu.make_async_copy(sources[k], held[k], sems.at[k]) for k in range(4)]
    for copy in copies:
        copy.start()
    for copy in copies:
        copy.wait()
    conv_ref, kv_ref, up_ref, down_ref = held

    def tiles(ref, count):
        return [ref[:, t * 128 : (t + 1) * 128].astype(F32) for t in range(count)]

    mlp = tiles(up_ref, 6) + tiles(down_ref, 6)

    def put(code):
        block = jnp.concatenate(code + mlp, axis=0).astype(BF)
        for k in range(16):
            out_ref[k] = block

    @pl.when(where_ref[0] == 0)
    def _():
        low, high = tiles(conv_ref, 2)
        half = jnp.where((where_ref[2] >> 1) == 0, low, high)
        put([half, jnp.zeros((6, 128), F32)])

    @pl.when(where_ref[0] != 0)
    def _():
        put(tiles(kv_ref, 12))


def kernel_call(body, out_shape, in_specs, scratch=(), out_specs=None):
    outs = out_specs or jax.tree.map(lambda _: VMEM, out_shape)
    return pl.pallas_call(
        body,
        out_shape=out_shape,
        in_specs=in_specs,
        out_specs=outs,
        scratch_shapes=scratch,
        compiler_params=pltpu.CompilerParams(vmem_limit_bytes=16 << 20),
    )


def in_hbm(value):
    return pltpu.with_memory_space_constraint(value, pltpu.HBM)


def by_core(even, odd):
    ids = np.arange(512).reshape(8, 2, 8, 4)
    groups = []
    for axes, views in ((even, (1, 3)), (odd, (0, 2))):
        held = [axis for axis in range(3) if axis not in axes]
        for view in views:
            lines = ids[..., view].transpose(*held, *axes)
            groups.extend(lines.reshape(-1, int(np.prod([ids.shape[a] for a in axes]))).tolist())
    return groups


def to_view(value, flip):
    return lax.ppermute(value, "view", [(i, i ^ flip) for i in range(4)])


def copies_of(value, count):
    return jnp.broadcast_to(value, (count, *value.shape))


def exchange(copies, groups):
    return lax.all_to_all(
        copies,
        ("dp", "slab_0", "slab_1", "view"),
        split_axis=0,
        concat_axis=0,
        axis_index_groups=groups,
        tiled=True,
    )


def regroup(tiles, rows):
    devices = tiles.shape[0]
    tiles = tiles.reshape(devices, -1, rows, 128).swapaxes(0, 1)
    return tiles.reshape(-1, 128)


def shards(
    latent_feats,
    conv_weight,
    kv_weight,
    stream,
    queries,
    norm_gain,
    up_weight,
    down_weight,
    band_start,
    band_end,
    visibility,
):
    view_id = lax.axis_index("view")
    core = 1 - view_id % 2
    first_row = lax.axis_index(SLAB) * 4
    where = jnp.stack([core, first_row, view_id]).astype(jnp.int32)
    feats = latent_feats[0, 0]
    ends = lax.axis_size(SLAB) - 1
    above = lax.ppermute(feats[2:], SLAB, [(i, i + 1) for i in range(ends)])
    below = lax.ppermute(feats[:2], SLAB, [(i + 1, i) for i in range(ends)])
    rows = jnp.concatenate([above, feats, below], axis=0).reshape(256, 256)
    even = core == 0
    mine = kernel_call(
        pack_kernel,
        jax.ShapeDtypeStruct((16, 96, 128), BF),
        [SMEM] + [HBM] * 4,
        scratch=[pltpu.VMEM(w.shape, BF) for w in (conv_weight, kv_weight, up_weight, down_weight)]
        + [pltpu.SemaphoreType.DMA((4,))],
    )(where, *map(in_hbm, (conv_weight, kv_weight, up_weight, down_weight)))
    wide = by_core((1, 2), (0, 1))
    long = by_core((0,), (2,))
    near = exchange(mine, wide)
    near, rows = lax.optimization_barrier((near, rows))
    code = jnp.where(
        even, jnp.pad(regroup(near[:, :18], 18), ((0, 96), (0, 0))), regroup(near[:, :24], 2)
    )
    units = jnp.concatenate([regroup(near[:, 24:60], 6), regroup(near[:, 60:], 6)], axis=0)
    code = copies_of(code, 8)
    own = exchange(code, long)
    rows = jnp.concatenate([rows, to_view(rows, 2)], axis=0)
    units = copies_of(units, 8)
    other = to_view(own, 1)
    mlp = exchange(units, long)

    encoded = kernel_call(
        conv_kernel,
        jax.ShapeDtypeStruct((384, 128), BF),
        [SMEM, HBM, VMEM, VMEM],
        scratch=[
            pltpu.VMEM((512, 256), BF),
            pltpu.SemaphoreType.DMA(()),
        ],
    )(where, in_hbm(rows), own, other)
    nearby = lax.all_gather(encoded, "view", axis=0, tiled=True)
    vis_row = lax.dynamic_index_in_dim(visibility[0], view_id, 0, False)
    seen = jnp.where(jnp.arange(4) == view_id, 1, vis_row).astype(jnp.int32)
    normed, residual = kernel_call(
        attention_kernel,
        (jax.ShapeDtypeStruct((128, 768), BF), pltpu.HBM((128, 768), F32)),
        [SMEM, SMEM, SMEM, SMEM] + [VMEM] * 6,
        scratch=[
            pltpu.VMEM((12, 768, 128), BF),
            pltpu.VMEM((128, 768), F32),
            pltpu.VMEM((128, 768), F32),
            pltpu.SemaphoreType.DMA((6,)),
        ],
        out_specs=(VMEM, HBM),
    )(
        where,
        band_start[0, 0],
        band_end[0, 0],
        seen,
        nearby,
        own,
        other,
        queries[0, 0].reshape(128, 768),
        stream[0, 0].reshape(128, 768),
        norm_gain.reshape(1, 768),
    )
    tokens = lax.all_gather(normed, "view", axis=0, tiled=True)
    tokens = kernel_call(
        swap_kernel, jax.ShapeDtypeStruct((512, 768), BF), [SMEM, VMEM]
    )(where, tokens)
    block = jax.ShapeDtypeStruct((128, 768), BF)
    square = jax.ShapeDtypeStruct((768, 768), BF)
    cross = kernel_call(cross_kernel, block, [SMEM, VMEM, VMEM])(where, tokens, mlp)
    cross = to_view(cross, 3)
    same = kernel_call(same_kernel, block, [SMEM, VMEM, VMEM])(where, tokens, mlp)
    same = to_view(same, 2)
    own, sibling, swap = kernel_call(
        near_kernel, (block, block, square), [SMEM, VMEM, VMEM]
    )(where, tokens, mlp)
    sibling = to_view(sibling, 1)
    result = kernel_call(
        sum_kernel, block, [SMEM] + [VMEM] * 6
    )(where, own, sibling, same, cross, swap, residual)
    return result.reshape(1, 1, 4, 32, 768)


def solution(mesh):
    finer = Mesh(
        mesh.devices.reshape(mesh.shape["dp"], 2, 8, mesh.shape["view"]),
        ("dp", "slab_0", "slab_1", "view"),
    )
    in_specs = (
        P("dp", "view", SLAB, None, None),
        P(DP_SLAB, None),
        P(DP_SLAB, None),
        P("dp", "view", SLAB, None, None),
        P("dp", "view", SLAB, None, None),
        P(),
        P(DP_SLAB, "view"),
        P(DP_SLAB, "view"),
        P("dp", "view", SLAB, None),
        P("dp", "view", SLAB, None),
        P("dp", None, None),
    )
    out_specs = P("dp", "view", SLAB, None, None)
    return jax.shard_map(
        shards, mesh=finer, in_specs=in_specs, out_specs=out_specs, check_vma=False
    )
```

profile of v0, /device:TPU:1, one launch (start us, length us, event | category | flops | bytes accessed | tf_op | source)
XLA Modules:
  0.0 116.7 jit_solution(9061848631847178474)
XLA Ops:
  0.1 2.1 %shard_map.109 = bf16[16,96,128]{2,1,0:T(8,128)(2,1)} custom-call(s32[3]{0:T(128)S(1)} %pad_add_fusion.where_ref, bf16[18,256]{1,0:T(8,128)(2,1)} %refs_0_.1, bf16[2,1536]{1,0:T(2,128)(2,1)} %refs_1_.1, bf16[6,768]{1,0:T(8,128)(2,1)} %refs_2_.1, bf16[6,768]{1,0:T(8,128)(2,1)} %refs_3_.1), custom_call_target="tpu_custom_call" | custom-call | tf_op jit(solution)/shard_map/pallas_call | solution.py:327
  2.2 13.4 %all-to-all-start = ((bf16[16,96,128]{2,1,0:T(8,128)(2,1)}), bf16[16,96,128]{2,1,0:T(8,128)(2,1)S(1)}, u32[]{:S(2)}, u32[]{:S(2)}) async-start(bf16[16,96,128]{2,1,0:T(8,128)(2,1)} %shard_map.109), calls=%async_computation | async-start | bytes 786432 | tf_op jit(solution)/shard_map/all_to_all | solution.py:288
  15.6 0.8 slice_bitcast_fusion.1
  16.4 3.3 %collective-permute-start = (bf16[2,32,256]{2,1,0:T(8,128)(2,1)S(1)}, bf16[2,32,256]{2,1,0:T(8,128)(2,1)S(1)}, u32[]{:S(2)}, u32[]{:S(2)}) collective-permute-start(bf16[2,32,256]{2,1,0:T(8,128)(2,1)S(1)} %get-tuple-element.21), channel_id=1, source_target_pairs={{0,4},{4,8},{8,12},{12,16},{16,20},{20,24},{24,28},{28,32},{32,36}... | collective-permute-start | bytes 98312 | tf_op jit(solution)/shard_map/ppermute | solution.py:323
  19.7 1.3 %collective-permute-start.1 = (bf16[2,32,256]{2,1,0:T(8,128)(2,1)S(1)}, bf16[2,32,256]{2,1,0:T(8,128)(2,1)S(1)}, u32[]{:S(2)}, u32[]{:S(2)}) collective-permute-start(bf16[2,32,256]{2,1,0:T(8,128)(2,1)S(1)} %get-tuple-element.22), channel_id=1, source_target_pairs={{4,0},{8,4},{12,8},{16,12},{20,16},{24,20},{28,24},{32,28},{36,32}... | collective-permute-start | bytes 98312 | tf_op jit(solution)/shard_map/ppermute | solution.py:324
  21.0 0.3 collective-permute-done
  21.3 3.4 %collective-permute-done.1 = bf16[2,32,256]{2,1,0:T(8,128)(2,1)S(1)} collective-permute-done((bf16[2,32,256]{2,1,0:T(8,128)(2,1)S(1)}, bf16[2,32,256]{2,1,0:T(8,128)(2,1)S(1)}, u32[]{:S(2)}, u32[]{:S(2)}) %collective-permute-start.1) | collective-permute-done | bytes 32800 | tf_op jit(solution)/shard_map/ppermute | solution.py:324
  24.6 1.5 %pad_maximum_fusion.2 = bf16[8,32,256]{2,1,0:T(8,128)(2,1)} fusion(bf16[2,32,256]{2,1,0:T(8,128)(2,1)S(1)} %collective-permute-done.1, bf16[4,32,256]{2,1,0:T(8,128)(2,1)} %bitcast.36, bf16[2,32,256]{2,1,0:T(8,128)(2,1)S(1)} %collective-permute-done), kind=kLoop, calls=%fused_computation.2 | loop fusion | flops 131072 | bytes 262144 | tf_op jit(solution)/shard_map/concatenate | solution.py:325
  26.6 1.0 broadcast_in_dim.11
  27.6 6.7 %all-to-all-start.1 = ((bf16[8,384,128]{2,1,0:T(8,128)(2,1)}), bf16[8,384,128]{2,1,0:T(8,128)(2,1)S(1)}, u32[]{:S(2)}, u32[]{:S(2)}) async-start(bf16[8,384,128]{2,1,0:T(8,128)(2,1)} %broadcast_in_dim.11), calls=%async_computation.1 | async-start | bytes 1572864 | tf_op jit(solution)/shard_map/all_to_all | solution.py:288
  34.7 14.6 %all-to-all-done.1.own_ref = bf16[8,384,128]{2,1,0:T(8,128)(2,1)S(1)} async-done(((bf16[8,384,128]{2,1,0:T(8,128)(2,1)}), bf16[8,384,128]{2,1,0:T(8,128)(2,1)S(1)}, u32[]{:S(2)}, u32[]{:S(2)}) %all-to-all-start.1) | async-done | bytes 786464 | tf_op jit(solution)/shard_map/all_to_all | solution.py:288
  49.3 1.8 %broadcast_in_dim.12 = bf16[8,1152,128]{2,1,0:T(8,128)(2,1)} broadcast(bf16[1152,128]{1,0:T(8,128)(2,1)S(1)} %pad_maximum_fusion), dimensions={1,2} | broadcast | bytes 2654208 | tf_op jit(solution)/shard_map/broadcast_in_dim | solution.py:284
  51.1 3.7 %all-to-all-start.2 = ((bf16[8,1152,128]{2,1,0:T(8,128)(2,1)}), bf16[8,1152,128]{2,1,0:T(8,128)(2,1)S(1)}, u32[]{:S(2)}, u32[]{:S(2)}) async-start(bf16[8,1152,128]{2,1,0:T(8,128)(2,1)} %broadcast_in_dim.12), calls=%async_computation.2 | async-start | bytes 4718592 | tf_op jit(solution)/shard_map/all_to_all | solution.py:288
  54.9 7.4 %collective-permute-start.3 = (bf16[8,384,128]{2,1,0:T(8,128)(2,1)S(1)}, bf16[8,384,128]{2,1,0:T(8,128)(2,1)}, u32[]{:S(2)}, u32[]{:S(2)}) collective-permute-start(bf16[8,384,128]{2,1,0:T(8,128)(2,1)S(1)} %all-to-all-done.1.own_ref), channel_id=1, source_target_pairs={{0,1},{1,0},{2,3},{3,2},{4,5},{5,4},{6,7},{7,6},{8,9},{9,8},{10,11... | collective-permute-start | bytes 2359304 | tf_op jit(solution)/shard_map/ppermute | solution.py:280
  62.3 2.2 %collective-permute-start.2 = (bf16[256,256]{1,0:T(8,128)(2,1)}, bf16[256,256]{1,0:T(8,128)(2,1)}, u32[]{:S(2)}, u32[]{:S(2)}) collective-permute-start(bf16[256,256]{1,0:T(8,128)(2,1)} %bitcast.32), channel_id=1, source_target_pairs={{0,2},{1,3},{2,0},{3,1},{4,6},{5,7},{6,4},{7,5},{8,10},{9,11},{10,... | collective-permute-start | bytes 393224 | tf_op jit(solution)/shard_map/ppermute | solution.py:280
  64.5 0.7 compare_select_fusion.seen_ref
  65.2 4.3 %collective-permute-done.2 = bf16[256,256]{1,0:T(8,128)(2,1)} collective-permute-done((bf16[256,256]{1,0:T(8,128)(2,1)}, bf16[256,256]{1,0:T(8,128)(2,1)}, u32[]{:S(2)}, u32[]{:S(2)}) %collective-permute-start.2) | collective-permute-done | bytes 131104 | tf_op jit(solution)/shard_map/ppermute | solution.py:280
  69.5 1.7 %pad_maximum_fusion.1.rows_ref = bf16[512,256]{1,0:T(8,128)(2,1)} fusion(bf16[256,256]{1,0:T(8,128)(2,1)} %collective-permute-done.2, bf16[256,256]{1,0:T(8,128)(2,1)} %bitcast.33), kind=kLoop, calls=%fused_computation.1 | loop fusion | flops 524288 | bytes 524288 | tf_op jit(solution)/shard_map/concatenate | solution.py:344
  71.2 2.9 %shard_map.110 = bf16[384,128]{1,0:T(8,128)(2,1)S(1)} custom-call(s32[3]{0:T(128)S(1)} %pad_add_fusion.where_ref, bf16[512,256]{1,0:T(8,128)(2,1)} %pad_maximum_fusion.1.rows_ref, bf16[8,384,128]{2,1,0:T(8,128)(2,1)S(1)} %all-to-all-done.1.own_ref, bf16[8,384,128]{2,1,0:T(8,128)(2,1)} %collective-permute-done.3.other_ref), custom_call_target="tpu_custom_call" | custom-call | tf_op jit(solution)/shard_map/pallas_call | solution.py:349
  74.1 6.9 %all_gather.6.enc_ref = bf16[1536,128]{1,0:T(8,128)(2,1)S(1)} all-gather(bf16[384,128]{1,0:T(8,128)(2,1)S(1)} %shard_map.110), channel_id=1, replica_groups=mesh['dp'=8,'slab_0'=2,'slab_1'=8,'view'=4] {'view'}, dimensions={0}, use_global_device_ids=true | all-gather | bytes 491520 | tf_op jit(solution)/shard_map/all_gather | solution.py:358
  81.0 5.5 %shard_map.111 = (bf16[128,768]{1,0:T(8,128)(2,1)S(1)}, f32[128,768]{1,0:T(8,128)}) custom-call(s32[3]{0:T(128)S(1)} %pad_add_fusion.where_ref, s32[4,4]{1,0:T(4,128)S(1)} %bitcast.28, s32[4,4]{1,0:T(4,128)S(1)} %bitcast.29, s32[4]{0:T(128)S(1)} %compare_select_fusion.seen_ref, bf16[1536,128]{1,0:T(8,128)(2,1)S(1)} %all_gather.6.enc_ref, ...), custom_call_target="tpu_custom_call" | custom-call | tf_op jit(solution)/shard_map/pallas_call | solution.py:361
  86.5 8.7 %all_gather.7.tok_ref = bf16[512,768]{1,0:T(8,128)(2,1)S(1)} all-gather(bf16[128,768]{1,0:T(8,128)(2,1)S(1)} %get-tuple-element.14), channel_id=1, replica_groups=mesh['dp'=8,'slab_0'=2,'slab_1'=8,'view'=4] {'view'}, dimensions={0}, use_global_device_ids=true | all-gather | bytes 983040 | tf_op jit(solution)/shard_map/all_gather | solution.py:384
  95.2 0.6 shard_map.112.tok_ref
  95.8 2.0 %shard_map.113 = (bf16[128,768]{1,0:T(8,128)(2,1)S(1)}, bf16[128,768]{1,0:T(8,128)(2,1)S(1)}, bf16[768,768]{1,0:T(8,128)(2,1)S(1)}) custom-call(s32[3]{0:T(128)S(1)} %pad_add_fusion.where_ref, bf16[512,768]{1,0:T(8,128)(2,1)S(1)} %shard_map.112.tok_ref, bf16[8,1152,128]{2,1,0:T(8,128)(2,1)S(1)} %all-to-all-done.2.w_ref), custom_call_target="tpu_custom_call" | custom-call | tf_op jit(solution)/shard_map/pallas_call | solution.py:394
  97.8 2.8 %collective-permute-start.4 = (bf16[128,768]{1,0:T(8,128)(2,1)S(1)}, bf16[128,768]{1,0:T(8,128)(2,1)S(1)}, u32[]{:S(2)}, u32[]{:S(2)}) collective-permute-start(bf16[128,768]{1,0:T(8,128)(2,1)S(1)} %get-tuple-element.16), channel_id=1, source_target_pairs={{0,1},{1,0},{2,3},{3,2},{4,5},{5,4},{6,7},{7,6},{8,9},{9,8},{10,11... | collective-permute-start | bytes 589832 | tf_op jit(solution)/shard_map/ppermute | solution.py:280
  100.7 1.3 %shard_map.114 = bf16[128,768]{1,0:T(8,128)(2,1)S(1)} custom-call(s32[3]{0:T(128)S(1)} %pad_add_fusion.where_ref, bf16[512,768]{1,0:T(8,128)(2,1)S(1)} %shard_map.112.tok_ref, bf16[8,1152,128]{2,1,0:T(8,128)(2,1)S(1)} %all-to-all-done.2.w_ref), custom_call_target="tpu_custom_call" | custom-call | tf_op jit(solution)/shard_map/pallas_call | solution.py:392
  102.0 2.6 %collective-permute-start.5 = (bf16[128,768]{1,0:T(8,128)(2,1)S(1)}, bf16[128,768]{1,0:T(8,128)(2,1)S(1)}, u32[]{:S(2)}, u32[]{:S(2)}) collective-permute-start(bf16[128,768]{1,0:T(8,128)(2,1)S(1)} %shard_map.114), channel_id=1, source_target_pairs={{0,2},{1,3},{2,0},{3,1},{4,6},{5,7},{6,4},{7,5},{8,10},{9,11},{10,... | collective-permute-start | bytes 589832 | tf_op jit(solution)/shard_map/ppermute | solution.py:280
  104.6 1.3 %shard_map.115 = bf16[128,768]{1,0:T(8,128)(2,1)S(1)} custom-call(s32[3]{0:T(128)S(1)} %pad_add_fusion.where_ref, bf16[512,768]{1,0:T(8,128)(2,1)S(1)} %shard_map.112.tok_ref, bf16[8,1152,128]{2,1,0:T(8,128)(2,1)S(1)} %all-to-all-done.2.w_ref), custom_call_target="tpu_custom_call" | custom-call | tf_op jit(solution)/shard_map/pallas_call | solution.py:390
  106.0 3.0 %collective-permute-start.6 = (bf16[128,768]{1,0:T(8,128)(2,1)S(1)}, bf16[128,768]{1,0:T(8,128)(2,1)S(1)}, u32[]{:S(2)}, u32[]{:S(2)}) collective-permute-start(bf16[128,768]{1,0:T(8,128)(2,1)S(1)} %shard_map.115), channel_id=1, source_target_pairs={{0,3},{1,2},{2,1},{3,0},{4,7},{5,6},{6,5},{7,4},{8,11},{9,10},{10,... | collective-permute-start | bytes 589832 | tf_op jit(solution)/shard_map/ppermute | solution.py:280
  109.0 1.5 %collective-permute-done.5.same_ref = bf16[128,768]{1,0:T(8,128)(2,1)S(1)} collective-permute-done((bf16[128,768]{1,0:T(8,128)(2,1)S(1)}, bf16[128,768]{1,0:T(8,128)(2,1)S(1)}, u32[]{:S(2)}, u32[]{:S(2)}) %collective-permute-start.5) | collective-permute-done | bytes 196640 | tf_op jit(solution)/shard_map/ppermute | solution.py:280
  110.5 4.5 %collective-permute-done.6.cross_ref = bf16[128,768]{1,0:T(8,128)(2,1)S(1)} collective-permute-done((bf16[128,768]{1,0:T(8,128)(2,1)S(1)}, bf16[128,768]{1,0:T(8,128)(2,1)S(1)}, u32[]{:S(2)}, u32[]{:S(2)}) %collective-permute-start.6) | collective-permute-done | bytes 196640 | tf_op jit(solution)/shard_map/ppermute | solution.py:280
  115.0 1.7 %shard_map.116 = bf16[128,768]{1,0:T(8,128)(2,1)} custom-call(s32[3]{0:T(128)S(1)} %pad_add_fusion.where_ref, bf16[128,768]{1,0:T(8,128)(2,1)S(1)} %get-tuple-element.15.own_ref, bf16[128,768]{1,0:T(8,128)(2,1)S(1)} %collective-permute-done.4.sibling_ref, bf16[128,768]{1,0:T(8,128)(2,1)S(1)} %collective-permute-done.5.same_ref, ...), custom_call_target="tpu_custom_call" | custom-call | tf_op jit(solution)/shard_map/pallas_call | solution.py:398
  (31 shorter events, 0.8 us)
Async XLA Ops:
  2.2 24.2 %all-to-all-start = ((bf16[16,96,128]{2,1,0:T(8,128)(2,1)}), bf16[16,96,128]{2,1,0:T(8,128)(2,1)S(1)}, u32[]{:S(2)}, u32[]{:S(2)}) async-start(bf16[16,96,128]{2,1,0:T(8,128)(2,1)} %shard_map.109), calls=%async_computation | async-start | bytes 786432 | tf_op jit(solution)/shard_map/all_to_all | solution.py:288
  16.4 4.9 %collective-permute-start = (bf16[2,32,256]{2,1,0:T(8,128)(2,1)S(1)}, bf16[2,32,256]{2,1,0:T(8,128)(2,1)S(1)}, u32[]{:S(2)}, u32[]{:S(2)}) collective-permute-start(bf16[2,32,256]{2,1,0:T(8,128)(2,1)S(1)} %get-tuple-element.21), channel_id=1, source_target_pairs={{0,4},{4,8},{8,12},{12,16},{16,20},{20,24},{24,28},{28,32},{32,36}... | collective-permute-start | bytes 98312 | tf_op jit(solution)/shard_map/ppermute | solution.py:323
  19.7 5.0 %collective-permute-start.1 = (bf16[2,32,256]{2,1,0:T(8,128)(2,1)S(1)}, bf16[2,32,256]{2,1,0:T(8,128)(2,1)S(1)}, u32[]{:S(2)}, u32[]{:S(2)}) collective-permute-start(bf16[2,32,256]{2,1,0:T(8,128)(2,1)S(1)} %get-tuple-element.22), channel_id=1, source_target_pairs={{4,0},{8,4},{12,8},{16,12},{20,16},{24,20},{28,24},{32,28},{36,32}... | collective-permute-start | bytes 98312 | tf_op jit(solution)/shard_map/ppermute | solution.py:324
  27.6 21.7 %all-to-all-start.1 = ((bf16[8,384,128]{2,1,0:T(8,128)(2,1)}), bf16[8,384,128]{2,1,0:T(8,128)(2,1)S(1)}, u32[]{:S(2)}, u32[]{:S(2)}) async-start(bf16[8,384,128]{2,1,0:T(8,128)(2,1)} %broadcast_in_dim.11), calls=%async_computation.1 | async-start | bytes 1572864 | tf_op jit(solution)/shard_map/all_to_all | solution.py:288
  51.1 13.4 %copy-start.5 = (f32[768]{0:T(1024)S(1)}, f32[768]{0:T(1024)}, u32[]{:S(2)}) copy-start(f32[768]{0:T(1024)} %param.16) | copy-start | bytes 9220
  51.1 44.8 %all-to-all-start.2 = ((bf16[8,1152,128]{2,1,0:T(8,128)(2,1)}), bf16[8,1152,128]{2,1,0:T(8,128)(2,1)S(1)}, u32[]{:S(2)}, u32[]{:S(2)}) async-start(bf16[8,1152,128]{2,1,0:T(8,128)(2,1)} %broadcast_in_dim.12), calls=%async_computation.2 | async-start | bytes 4718592 | tf_op jit(solution)/shard_map/all_to_all | solution.py:288
  54.8 26.2 %copy-start.1 = (bf16[1,1,4,32,768]{4,3,2,1,0:T(8,128)(2,1)S(1)}, bf16[1,1,4,32,768]{4,3,2,1,0:T(8,128)(2,1)}, u32[]{:S(2)}) copy-start(bf16[1,1,4,32,768]{4,3,2,1,0:T(8,128)(2,1)} %param.15) | copy-start | bytes 589828
  54.8 26.1 %copy-start.2 = (bf16[1,1,4,32,768]{4,3,2,1,0:T(8,128)(2,1)S(1)}, bf16[1,1,4,32,768]{4,3,2,1,0:T(8,128)(2,1)}, u32[]{:S(2)}) copy-start(bf16[1,1,4,32,768]{4,3,2,1,0:T(8,128)(2,1)} %param.14) | copy-start | bytes 589828
  54.8 26.1 %copy-start.3 = (s32[1,1,4,4]{3,2,1,0:T(4,128)S(1)}, s32[1,1,4,4]{3,2,1,0:T(4,128)}, u32[]{:S(2)}) copy-start(s32[1,1,4,4]{3,2,1,0:T(4,128)} %param.19) | copy-start | bytes 196
  54.9 26.1 %copy-start.4 = (s32[1,1,4,4]{3,2,1,0:T(4,128)S(1)}, s32[1,1,4,4]{3,2,1,0:T(4,128)}, u32[]{:S(2)}) copy-start(s32[1,1,4,4]{3,2,1,0:T(4,128)} %param.20) | copy-start | bytes 196
  54.9 16.3 %collective-permute-start.3 = (bf16[8,384,128]{2,1,0:T(8,128)(2,1)S(1)}, bf16[8,384,128]{2,1,0:T(8,128)(2,1)}, u32[]{:S(2)}, u32[]{:S(2)}) collective-permute-start(bf16[8,384,128]{2,1,0:T(8,128)(2,1)S(1)} %all-to-all-done.1.own_ref), channel_id=1, source_target_pairs={{0,1},{1,0},{2,3},{3,2},{4,5},{5,4},{6,7},{7,6},{8,9},{9,8},{10,11... | collective-permute-start | bytes 2359304 | tf_op jit(solution)/shard_map/ppermute | solution.py:280
  62.3 7.3 %collective-permute-start.2 = (bf16[256,256]{1,0:T(8,128)(2,1)}, bf16[256,256]{1,0:T(8,128)(2,1)}, u32[]{:S(2)}, u32[]{:S(2)}) collective-permute-start(bf16[256,256]{1,0:T(8,128)(2,1)} %bitcast.32), channel_id=1, source_target_pairs={{0,2},{1,3},{2,0},{3,1},{4,6},{5,7},{6,4},{7,5},{8,10},{9,11},{10,... | collective-permute-start | bytes 393224 | tf_op jit(solution)/shard_map/ppermute | solution.py:280
  97.8 11.1 %collective-permute-start.4 = (bf16[128,768]{1,0:T(8,128)(2,1)S(1)}, bf16[128,768]{1,0:T(8,128)(2,1)S(1)}, u32[]{:S(2)}, u32[]{:S(2)}) collective-permute-start(bf16[128,768]{1,0:T(8,128)(2,1)S(1)} %get-tuple-element.16), channel_id=1, source_target_pairs={{0,1},{1,0},{2,3},{3,2},{4,5},{5,4},{6,7},{7,6},{8,9},{9,8},{10,11... | collective-permute-start | bytes 589832 | tf_op jit(solution)/shard_map/ppermute | solution.py:280
  102.0 13.0 %copy-start = (f32[128,768]{1,0:T(8,128)S(1)}, f32[128,768]{1,0:T(8,128)}, u32[]{:S(2)}) copy-start(f32[128,768]{1,0:T(8,128)} %get-tuple-element.18.residual_ref) | copy-start | bytes 1179652
  102.0 8.5 %collective-permute-start.5 = (bf16[128,768]{1,0:T(8,128)(2,1)S(1)}, bf16[128,768]{1,0:T(8,128)(2,1)S(1)}, u32[]{:S(2)}, u32[]{:S(2)}) collective-permute-start(bf16[128,768]{1,0:T(8,128)(2,1)S(1)} %shard_map.114), channel_id=1, source_target_pairs={{0,2},{1,3},{2,0},{3,1},{4,6},{5,7},{6,4},{7,5},{8,10},{9,11},{10,... | collective-permute-start | bytes 589832 | tf_op jit(solution)/shard_map/ppermute | solution.py:280
  106.0 9.0 %collective-permute-start.6 = (bf16[128,768]{1,0:T(8,128)(2,1)S(1)}, bf16[128,768]{1,0:T(8,128)(2,1)S(1)}, u32[]{:S(2)}, u32[]{:S(2)}) collective-permute-start(bf16[128,768]{1,0:T(8,128)(2,1)S(1)} %shard_map.115), channel_id=1, source_target_pairs={{0,3},{1,2},{2,1},{3,0},{4,7},{5,6},{6,5},{7,4},{8,11},{9,10},{10,... | collective-permute-start | bytes 589832 | tf_op jit(solution)/shard_map/ppermute | solution.py:280
where the time goes:
time: 118 us; the launch traced here: 117 us
  starting transfers between devices  46.5 us (39%)
  waiting for transfers between devices  28.8 us (24%)
  Pallas kernels  17.5 us (15%)
  blocking collectives  15.6 us (13%)
  other arithmetic  4.01 us (3%)
  local copies, waits for them, and re-layouts  4 us (3%)
    all_to_all x3, starting transfers between devices, exchange(): lax.all_to_all(copies, ('dp', 'slab_0', 'slab_1', 'view'), split_axis=0,...  23.9 us
    ppermute x5, starting transfers between devices, to_view(): return lax.ppermute(value, 'view', [(i, i ^ flip) for i in range(4)])  18.1 us
    all_to_all x3, waiting for transfers between devices, exchange(): lax.all_to_all(copies, ('dp', 'slab_0', 'slab_1', 'view'), split_axis=0,...  14.8 us
    ppermute x5, waiting for transfers between devices, to_view(): return lax.ppermute(value, 'view', [(i, i ^ flip) for i in range(4)])  10.3 us
    all_gather x1, blocking collectives, shards(): tokens = lax.all_gather(normed, 'view', axis=0, tiled=True)  8.71 us
    all_gather x1, blocking collectives, shards(): nearby = lax.all_gather(encoded, 'view', axis=0, tiled=True)  6.85 us
    pallas_call x1, Pallas kernels, shards(): kernel_call(attention_kernel, (jax.ShapeDtypeStruct((128, 768), BF), pltp...  5.5 us
    ppermute x1, waiting for transfers between devices, shards(): below = lax.ppermute(feats[:2], SLAB, [(i + 1, i) for i in range(ends)])  3.36 us
  transfers between devices with their start and end apart: 10, of which 7 were waited for; matrix products, arithmetic and copies ran while one was open for 4% of the time, Pallas kernels for 10%

commit v1 on v0

--- a/solution.py
+++ b/solution.py
@@ -157,9 +157,9 @@
     return 0.5 * v * (1.0 + jnp.tanh(0.7978845608028654 * (v + 0.044715 * (v * v * v))))
 
 
-def blocks_of(where_ref, tok_ref, w_ref, out_refs, chip_flip, flips):
+def two_blocks(where_ref, tok_ref, w_ref, out_refs, chip_flip):
     blocks = []
-    for flip in flips:
+    for flip in range(2):
         view = where_ref[2] ^ (chip_flip * 2 + flip)
         blocks.append(tok_ref[pl.ds(pl.multiple_of(view * 128, 128), 128), :])
 
@@ -177,16 +177,12 @@
         out_ref[...] = parts[k * 128 : (k + 1) * 128]
 
 
-def cross_kernel(where_ref, tok_ref, w_ref, cross_ref):
-    blocks_of(where_ref, tok_ref, w_ref, (cross_ref,), 1, (1,))
-
-
-def same_kernel(where_ref, tok_ref, w_ref, same_ref):
-    blocks_of(where_ref, tok_ref, w_ref, (same_ref,), 1, (0,))
+def far_kernel(where_ref, tok_ref, w_ref, same_ref, cross_ref):
+    two_blocks(where_ref, tok_ref, w_ref, (same_ref, cross_ref), 1)
 
 
 def near_kernel(where_ref, tok_ref, w_ref, own_ref, sibling_ref, swap_ref):
-    blocks_of(where_ref, tok_ref, w_ref, (own_ref, sibling_ref), 0, (0, 1))
+    two_blocks(where_ref, tok_ref, w_ref, (own_ref, sibling_ref), 0)
     swap_ref[...] = one_hot(768, 6)
 
 
@@ -268,7 +264,7 @@
 def by_core(even, odd):
     ids = np.arange(512).reshape(8, 2, 8, 4)
     groups = []
-    for axes, views in ((even, (1, 3)), (odd, (0, 2))):
+    for axes, views in ((even, (0, 2)), (odd, (1, 3))):
         held = [axis for axis in range(3) if axis not in axes]
         for view in views:
             lines = ids[..., view].transpose(*held, *axes)
@@ -315,7 +311,7 @@
     visibility,
 ):
     view_id = lax.axis_index("view")
-    core = 1 - view_id % 2
+    core = view_id % 2
     first_row = lax.axis_index(SLAB) * 4
     where = jnp.stack([core, first_row, view_id]).astype(jnp.int32)
     feats = latent_feats[0, 0]
@@ -334,7 +330,6 @@
     wide = by_core((1, 2), (0, 1))
     long = by_core((0,), (2,))
     near = exchange(mine, wide)
-    near, rows = lax.optimization_barrier((near, rows))
     code = jnp.where(
         even, jnp.pad(regroup(near[:, :18], 18), ((0, 96), (0, 0))), regroup(near[:, :24], 2)
     )
@@ -387,9 +382,8 @@
     )(where, tokens)
     block = jax.ShapeDtypeStruct((128, 768), BF)
     square = jax.ShapeDtypeStruct((768, 768), BF)
-    cross = kernel_call(cross_kernel, block, [SMEM, VMEM, VMEM])(where, tokens, mlp)
+    same, cross = kernel_call(far_kernel, (block, block), [SMEM, VMEM, VMEM])(where, tokens, mlp)
     cross = to_view(cross, 3)
-    same = kernel_call(same_kernel, block, [SMEM, VMEM, VMEM])(where, tokens, mlp)
     same = to_view(same, 2)
     own, sibling, swap = kernel_call(
         near_kernel, (block, block, square), [SMEM, VMEM, VMEM]

time: 118 us -> 136 us (1.15)
  waiting for transfers between devices: 28.8 us -> 53.2 us
  starting transfers between devices: 46.5 us -> 42 us
    ppermute x1, waiting for transfers between devices: 0.28 us -> 14.7 us  [shards(): above = lax.ppermute(feats[2:], SLAB, [(i, i + 1) for i in range(ends)])]
    all_to_all x3, waiting for transfers between devices: 14.8 us -> 27.2 us  [exchange(): lax.all_to_all(copies, ('dp', 'slab_0', 'slab_1', 'view'), split_axis=0,...]
    ppermute x5, starting transfers between devices: 18.1 us -> 13.6 us  [to_view(): return lax.ppermute(value, 'view', [(i, i ^ flip) for i in range(4)])]
    ppermute x5, waiting for transfers between devices: 10.3 us -> 6.18 us  [to_view(): return lax.ppermute(value, 'view', [(i, i ^ flip) for i in range(4)])]
    ppermute x1, waiting for transfers between devices: 3.36 us -> 5.19 us  [shards(): below = lax.ppermute(feats[:2], SLAB, [(i + 1, i) for i in range(ends)])]
  transfers between devices with their start and end apart: 10 -> 10, of which waited for: 7 -> 6; matrix products, arithmetic and copies ran while one was open for 4% -> 4% of each run, Pallas kernels for 10% -> 9%
where the time goes in v1:
time: 136 us; the launch traced here: 135 us
  waiting for transfers between devices  53.2 us (39%)
  starting transfers between devices  42 us (31%)
  Pallas kernels  17.2 us (13%)
  blocking collectives  14.3 us (11%)
  other arithmetic  4 us (3%)
  local copies, waits for them, and re-layouts  3.99 us (3%)
    all_to_all x3, waiting for transfers between devices, exchange(): lax.all_to_all(copies, ('dp', 'slab_0', 'slab_1', 'view'), split_axis=0,...  27.2 us
    all_to_all x3, starting transfers between devices, exchange(): lax.all_to_all(copies, ('dp', 'slab_0', 'slab_1', 'view'), split_axis=0,...  24 us
    ppermute x1, waiting for transfers between devices, shards(): above = lax.ppermute(feats[2:], SLAB, [(i, i + 1) for i in range(ends)])  14.7 us
    ppermute x5, starting transfers between devices, to_view(): return lax.ppermute(value, 'view', [(i, i ^ flip) for i in range(4)])  13.6 us
    all_gather x1, blocking collectives, shards(): tokens = lax.all_gather(normed, 'view', axis=0, tiled=True)  8.71 us
    ppermute x5, waiting for transfers between devices, to_view(): return lax.ppermute(value, 'view', [(i, i ^ flip) for i in range(4)])  6.18 us
    all_gather x1, blocking collectives, shards(): nearby = lax.all_gather(encoded, 'view', axis=0, tiled=True)  5.61 us
    pallas_call x1, Pallas kernels, shards(): kernel_call(attention_kernel, (jax.ShapeDtypeStruct((128, 768), BF), pltp...  5.56 us
  transfers between devices with their start and end apart: 10, of which 6 were waited for; matrix products, arithmetic and copies ran while one was open for 4% of the time, Pallas kernels for 9%

profile of v1, /device:TPU:1, one launch (start us, length us, event | category | flops | bytes accessed | tf_op | source)
XLA Modules:
  0.0 135.1 jit_solution(13233879070110491450)
XLA Ops:
  0.0 0.1 pad_add_fusion.where_ref
  0.1 2.1 %shard_map.109 = bf16[16,96,128]{2,1,0:T(8,128)(2,1)} custom-call(s32[3]{0:T(128)S(1)} %pad_add_fusion.where_ref, bf16[18,256]{1,0:T(8,128)(2,1)} %refs_0_.1, bf16[2,1536]{1,0:T(2,128)(2,1)} %refs_1_.1, bf16[6,768]{1,0:T(8,128)(2,1)} %refs_2_.1, bf16[6,768]{1,0:T(8,128)(2,1)} %refs_3_.1), custom_call_target="tpu_custom_call" | custom-call | tf_op jit(solution)/shard_map/pallas_call | solution.py:323
  2.2 10.2 %all-to-all-start = ((bf16[16,96,128]{2,1,0:T(8,128)(2,1)}), bf16[16,96,128]{2,1,0:T(8,128)(2,1)S(1)}, u32[]{:S(2)}, u32[]{:S(2)}) async-start(bf16[16,96,128]{2,1,0:T(8,128)(2,1)} %shard_map.109), calls=%async_computation | async-start | bytes 786432 | tf_op jit(solution)/shard_map/all_to_all | solution.py:284
  12.4 12.3 %all-to-all-done = bf16[16,96,128]{2,1,0:T(8,128)(2,1)S(1)} async-done(((bf16[16,96,128]{2,1,0:T(8,128)(2,1)}), bf16[16,96,128]{2,1,0:T(8,128)(2,1)S(1)}, u32[]{:S(2)}, u32[]{:S(2)}) %all-to-all-start) | async-done | bytes 393248 | tf_op jit(solution)/shard_map/all_to_all | solution.py:284
  24.9 1.0 broadcast_in_dim.11
  25.9 10.0 %all-to-all-start.1 = ((bf16[8,384,128]{2,1,0:T(8,128)(2,1)}), bf16[8,384,128]{2,1,0:T(8,128)(2,1)S(1)}, u32[]{:S(2)}, u32[]{:S(2)}) async-start(bf16[8,384,128]{2,1,0:T(8,128)(2,1)} %broadcast_in_dim.11), calls=%async_computation.1 | async-start | bytes 1572864 | tf_op jit(solution)/shard_map/all_to_all | solution.py:284
  36.3 14.9 %all-to-all-done.1.own_ref = bf16[8,384,128]{2,1,0:T(8,128)(2,1)S(1)} async-done(((bf16[8,384,128]{2,1,0:T(8,128)(2,1)}), bf16[8,384,128]{2,1,0:T(8,128)(2,1)S(1)}, u32[]{:S(2)}, u32[]{:S(2)}) %all-to-all-start.1) | async-done | bytes 786464 | tf_op jit(solution)/shard_map/all_to_all | solution.py:284
  51.2 1.7 %broadcast_in_dim.12 = bf16[8,1152,128]{2,1,0:T(8,128)(2,1)} broadcast(bf16[1152,128]{1,0:T(8,128)(2,1)S(1)} %pad_maximum_fusion), dimensions={1,2} | broadcast | bytes 2654208 | tf_op jit(solution)/shard_map/broadcast_in_dim | solution.py:280
  52.9 3.7 %all-to-all-start.2 = ((bf16[8,1152,128]{2,1,0:T(8,128)(2,1)}), bf16[8,1152,128]{2,1,0:T(8,128)(2,1)S(1)}, u32[]{:S(2)}, u32[]{:S(2)}) async-start(bf16[8,1152,128]{2,1,0:T(8,128)(2,1)} %broadcast_in_dim.12), calls=%async_computation.2 | async-start | bytes 4718592 | tf_op jit(solution)/shard_map/all_to_all | solution.py:284
  56.7 3.7 %collective-permute-start.3 = (bf16[8,384,128]{2,1,0:T(8,128)(2,1)S(1)}, bf16[8,384,128]{2,1,0:T(8,128)(2,1)}, u32[]{:S(2)}, u32[]{:S(2)}) collective-permute-start(bf16[8,384,128]{2,1,0:T(8,128)(2,1)S(1)} %all-to-all-done.1.own_ref), channel_id=1, source_target_pairs={{0,1},{1,0},{2,3},{3,2},{4,5},{5,4},{6,7},{7,6},{8,9},{9,8},{10,11... | collective-permute-start | bytes 2359304 | tf_op jit(solution)/shard_map/ppermute | solution.py:276
  60.4 0.8 slice_bitcast_fusion.1
  61.2 3.1 %collective-permute-start = (bf16[2,32,256]{2,1,0:T(8,128)(2,1)S(1)}, bf16[2,32,256]{2,1,0:T(8,128)(2,1)S(1)}, u32[]{:S(2)}, u32[]{:S(2)}) collective-permute-start(bf16[2,32,256]{2,1,0:T(8,128)(2,1)S(1)} %get-tuple-element.21), channel_id=1, source_target_pairs={{0,4},{4,8},{8,12},{12,16},{16,20},{20,24},{24,28},{28,32},{32,36}... | collective-permute-start | bytes 98312 | tf_op jit(solution)/shard_map/ppermute | solution.py:319
  64.3 1.3 collective-permute-start.1
  65.6 14.7 %collective-permute-done = bf16[2,32,256]{2,1,0:T(8,128)(2,1)S(1)} collective-permute-done((bf16[2,32,256]{2,1,0:T(8,128)(2,1)S(1)}, bf16[2,32,256]{2,1,0:T(8,128)(2,1)S(1)}, u32[]{:S(2)}, u32[]{:S(2)}) %collective-permute-start) | collective-permute-done | bytes 32800 | tf_op jit(solution)/shard_map/ppermute | solution.py:319
  80.3 5.2 %collective-permute-done.1 = bf16[2,32,256]{2,1,0:T(8,128)(2,1)S(1)} collective-permute-done((bf16[2,32,256]{2,1,0:T(8,128)(2,1)S(1)}, bf16[2,32,256]{2,1,0:T(8,128)(2,1)S(1)}, u32[]{:S(2)}, u32[]{:S(2)}) %collective-permute-start.1) | collective-permute-done | bytes 32800 | tf_op jit(solution)/shard_map/ppermute | solution.py:320
  85.5 1.5 %pad_maximum_fusion.2 = bf16[8,32,256]{2,1,0:T(8,128)(2,1)} fusion(bf16[2,32,256]{2,1,0:T(8,128)(2,1)S(1)} %collective-permute-done.1, bf16[4,32,256]{2,1,0:T(8,128)(2,1)} %bitcast.34, bf16[2,32,256]{2,1,0:T(8,128)(2,1)S(1)} %collective-permute-done), kind=kLoop, calls=%fused_computation.2 | loop fusion | flops 131072 | bytes 262144 | tf_op jit(solution)/shard_map/concatenate | solution.py:321
  87.0 2.2 %collective-permute-start.2 = (bf16[256,256]{1,0:T(8,128)(2,1)}, bf16[256,256]{1,0:T(8,128)(2,1)}, u32[]{:S(2)}, u32[]{:S(2)}) collective-permute-start(bf16[256,256]{1,0:T(8,128)(2,1)} %bitcast.9), channel_id=1, source_target_pairs={{0,2},{1,3},{2,0},{3,1},{4,6},{5,7},{6,4},{7,5},{8,10},{9,11},{10,... | collective-permute-start | bytes 393224 | tf_op jit(solution)/shard_map/ppermute | solution.py:276
  89.3 0.7 compare_select_fusion.seen_ref
  90.0 3.1 %collective-permute-done.2 = bf16[256,256]{1,0:T(8,128)(2,1)} collective-permute-done((bf16[256,256]{1,0:T(8,128)(2,1)}, bf16[256,256]{1,0:T(8,128)(2,1)}, u32[]{:S(2)}, u32[]{:S(2)}) %collective-permute-start.2) | collective-permute-done | bytes 131104 | tf_op jit(solution)/shard_map/ppermute | solution.py:276
  93.0 1.7 %pad_maximum_fusion.1.rows_ref = bf16[512,256]{1,0:T(8,128)(2,1)} fusion(bf16[256,256]{1,0:T(8,128)(2,1)} %collective-permute-done.2, bf16[256,256]{1,0:T(8,128)(2,1)} %bitcast.9), kind=kLoop, calls=%fused_computation.1 | loop fusion | flops 524288 | bytes 524288 | tf_op jit(solution)/shard_map/concatenate | solution.py:339
  94.7 2.9 %shard_map.110 = bf16[384,128]{1,0:T(8,128)(2,1)S(1)} custom-call(s32[3]{0:T(128)S(1)} %pad_add_fusion.where_ref, bf16[512,256]{1,0:T(8,128)(2,1)} %pad_maximum_fusion.1.rows_ref, bf16[8,384,128]{2,1,0:T(8,128)(2,1)S(1)} %all-to-all-done.1.own_ref, bf16[8,384,128]{2,1,0:T(8,128)(2,1)} %collective-permute-done.3.other_ref), custom_call_target="tpu_custom_call" | custom-call | tf_op jit(solution)/shard_map/pallas_call | solution.py:344
  97.6 5.6 %all_gather.6.enc_ref = bf16[1536,128]{1,0:T(8,128)(2,1)S(1)} all-gather(bf16[384,128]{1,0:T(8,128)(2,1)S(1)} %shard_map.110), channel_id=1, replica_groups=mesh['dp'=8,'slab_0'=2,'slab_1'=8,'view'=4] {'view'}, dimensions={0}, use_global_device_ids=true | all-gather | bytes 491520 | tf_op jit(solution)/shard_map/all_gather | solution.py:353
  103.3 5.6 %shard_map.111 = (bf16[128,768]{1,0:T(8,128)(2,1)S(1)}, f32[128,768]{1,0:T(8,128)}) custom-call(s32[3]{0:T(128)S(1)} %pad_add_fusion.where_ref, s32[4,4]{1,0:T(4,128)S(1)} %bitcast.28, s32[4,4]{1,0:T(4,128)S(1)} %bitcast.29, s32[4]{0:T(128)S(1)} %compare_select_fusion.seen_ref, bf16[1536,128]{1,0:T(8,128)(2,1)S(1)} %all_gather.6.enc_ref, ...), custom_call_target="tpu_custom_call" | custom-call | tf_op jit(solution)/shard_map/pallas_call | solution.py:356
  108.8 8.7 %all_gather.7.tok_ref = bf16[512,768]{1,0:T(8,128)(2,1)S(1)} all-gather(bf16[128,768]{1,0:T(8,128)(2,1)S(1)} %get-tuple-element.12), channel_id=1, replica_groups=mesh['dp'=8,'slab_0'=2,'slab_1'=8,'view'=4] {'view'}, dimensions={0}, use_global_device_ids=true | all-gather | bytes 983040 | tf_op jit(solution)/shard_map/all_gather | solution.py:379
  117.5 1.4 %shard_map.112.tok_ref = bf16[512,768]{1,0:T(8,128)(2,1)S(1)} custom-call(s32[3]{0:T(128)S(1)} %pad_add_fusion.where_ref, bf16[512,768]{1,0:T(8,128)(2,1)S(1)} %all_gather.7.tok_ref), custom_call_target="tpu_custom_call" | custom-call | tf_op jit(solution)/shard_map/pallas_call | solution.py:380
  118.9 1.5 %shard_map.114 = (bf16[128,768]{1,0:T(8,128)(2,1)S(1)}, bf16[128,768]{1,0:T(8,128)(2,1)S(1)}) custom-call(s32[3]{0:T(128)S(1)} %pad_add_fusion.where_ref, bf16[512,768]{1,0:T(8,128)(2,1)S(1)} %shard_map.112.tok_ref, bf16[8,1152,128]{2,1,0:T(8,128)(2,1)S(1)} %all-to-all-done.2.w_ref), custom_call_target="tpu_custom_call" | custom-call | tf_op jit(solution)/shard_map/pallas_call | solution.py:385
  120.4 3.3 %collective-permute-start.5 = (bf16[128,768]{1,0:T(8,128)(2,1)S(1)}, bf16[128,768]{1,0:T(8,128)(2,1)S(1)}, u32[]{:S(2)}, u32[]{:S(2)}) collective-permute-start(bf16[128,768]{1,0:T(8,128)(2,1)S(1)} %get-tuple-element.15), channel_id=1, source_target_pairs={{0,2},{1,3},{2,0},{3,1},{4,6},{5,7},{6,4},{7,5},{8,10},{9,11},{10,... | collective-permute-start | bytes 589832 | tf_op jit(solution)/shard_map/ppermute | solution.py:276
  123.8 1.9 %collective-permute-start.6 = (bf16[128,768]{1,0:T(8,128)(2,1)S(1)}, bf16[128,768]{1,0:T(8,128)(2,1)S(1)}, u32[]{:S(2)}, u32[]{:S(2)}) collective-permute-start(bf16[128,768]{1,0:T(8,128)(2,1)S(1)} %get-tuple-element.16), channel_id=1, source_target_pairs={{0,3},{1,2},{2,1},{3,0},{4,7},{5,6},{6,5},{7,4},{8,11},{9,10},{10,... | collective-permute-start | bytes 589832 | tf_op jit(solution)/shard_map/ppermute | solution.py:276
  125.7 2.0 %shard_map.113 = (bf16[128,768]{1,0:T(8,128)(2,1)S(1)}, bf16[128,768]{1,0:T(8,128)(2,1)S(1)}, bf16[768,768]{1,0:T(8,128)(2,1)S(1)}) custom-call(s32[3]{0:T(128)S(1)} %pad_add_fusion.where_ref, bf16[512,768]{1,0:T(8,128)(2,1)S(1)} %shard_map.112.tok_ref, bf16[8,1152,128]{2,1,0:T(8,128)(2,1)S(1)} %all-to-all-done.2.w_ref), custom_call_target="tpu_custom_call" | custom-call | tf_op jit(solution)/shard_map/pallas_call | solution.py:388
  127.7 2.5 %collective-permute-start.4 = (bf16[128,768]{1,0:T(8,128)(2,1)S(1)}, bf16[128,768]{1,0:T(8,128)(2,1)S(1)}, u32[]{:S(2)}, u32[]{:S(2)}) collective-permute-start(bf16[128,768]{1,0:T(8,128)(2,1)S(1)} %get-tuple-element.14), channel_id=1, source_target_pairs={{0,1},{1,0},{2,3},{3,2},{4,5},{5,4},{6,7},{7,6},{8,9},{9,8},{10,11... | collective-permute-start | bytes 589832 | tf_op jit(solution)/shard_map/ppermute | solution.py:276
  130.2 3.1 %collective-permute-done.6.cross_ref = bf16[128,768]{1,0:T(8,128)(2,1)S(1)} collective-permute-done((bf16[128,768]{1,0:T(8,128)(2,1)S(1)}, bf16[128,768]{1,0:T(8,128)(2,1)S(1)}, u32[]{:S(2)}, u32[]{:S(2)}) %collective-permute-start.6) | collective-permute-done | bytes 196640 | tf_op jit(solution)/shard_map/ppermute | solution.py:276
  133.3 1.8 %shard_map.115 = bf16[128,768]{1,0:T(8,128)(2,1)} custom-call(s32[3]{0:T(128)S(1)} %pad_add_fusion.where_ref, bf16[128,768]{1,0:T(8,128)(2,1)S(1)} %get-tuple-element.13.own_ref, bf16[128,768]{1,0:T(8,128)(2,1)S(1)} %collective-permute-done.4.sibling_ref, bf16[128,768]{1,0:T(8,128)(2,1)S(1)} %collective-permute-done.5.same_ref, ...), custom_call_target="tpu_custom_call" | custom-call | tf_op jit(solution)/shard_map/pallas_call | solution.py:392
  (30 shorter events, 0.5 us)
Async XLA Ops:
  2.2 22.5 %all-to-all-start = ((bf16[16,96,128]{2,1,0:T(8,128)(2,1)}), bf16[16,96,128]{2,1,0:T(8,128)(2,1)S(1)}, u32[]{:S(2)}, u32[]{:S(2)}) async-start(bf16[16,96,128]{2,1,0:T(8,128)(2,1)} %shard_map.109), calls=%async_computation | async-start | bytes 786432 | tf_op jit(solution)/shard_map/all_to_all | solution.py:284
  25.9 25.3 %all-to-all-start.1 = ((bf16[8,384,128]{2,1,0:T(8,128)(2,1)}), bf16[8,384,128]{2,1,0:T(8,128)(2,1)S(1)}, u32[]{:S(2)}, u32[]{:S(2)}) async-start(bf16[8,384,128]{2,1,0:T(8,128)(2,1)} %broadcast_in_dim.11), calls=%async_computation.1 | async-start | bytes 1572864 | tf_op jit(solution)/shard_map/all_to_all | solution.py:284
  52.9 36.3 %copy-start.5 = (f32[768]{0:T(1024)S(1)}, f32[768]{0:T(1024)}, u32[]{:S(2)}) copy-start(f32[768]{0:T(1024)} %param.16) | copy-start | bytes 9220
  52.9 66.0 %all-to-all-start.2 = ((bf16[8,1152,128]{2,1,0:T(8,128)(2,1)}), bf16[8,1152,128]{2,1,0:T(8,128)(2,1)S(1)}, u32[]{:S(2)}, u32[]{:S(2)}) async-start(bf16[8,1152,128]{2,1,0:T(8,128)(2,1)} %broadcast_in_dim.12), calls=%async_computation.2 | async-start | bytes 4718592 | tf_op jit(solution)/shard_map/all_to_all | solution.py:284
  56.7 46.6 %copy-start.1 = (bf16[1,1,4,32,768]{4,3,2,1,0:T(8,128)(2,1)S(1)}, bf16[1,1,4,32,768]{4,3,2,1,0:T(8,128)(2,1)}, u32[]{:S(2)}) copy-start(bf16[1,1,4,32,768]{4,3,2,1,0:T(8,128)(2,1)} %param.15) | copy-start | bytes 589828
  56.7 46.6 %copy-start.2 = (bf16[1,1,4,32,768]{4,3,2,1,0:T(8,128)(2,1)S(1)}, bf16[1,1,4,32,768]{4,3,2,1,0:T(8,128)(2,1)}, u32[]{:S(2)}) copy-start(bf16[1,1,4,32,768]{4,3,2,1,0:T(8,128)(2,1)} %param.14) | copy-start | bytes 589828
  56.7 46.6 %copy-start.3 = (s32[1,1,4,4]{3,2,1,0:T(4,128)S(1)}, s32[1,1,4,4]{3,2,1,0:T(4,128)}, u32[]{:S(2)}) copy-start(s32[1,1,4,4]{3,2,1,0:T(4,128)} %param.19) | copy-start | bytes 196
  56.7 46.5 %copy-start.4 = (s32[1,1,4,4]{3,2,1,0:T(4,128)S(1)}, s32[1,1,4,4]{3,2,1,0:T(4,128)}, u32[]{:S(2)}) copy-start(s32[1,1,4,4]{3,2,1,0:T(4,128)} %param.20) | copy-start | bytes 196
  56.7 38.0 %collective-permute-start.3 = (bf16[8,384,128]{2,1,0:T(8,128)(2,1)S(1)}, bf16[8,384,128]{2,1,0:T(8,128)(2,1)}, u32[]{:S(2)}, u32[]{:S(2)}) collective-permute-start(bf16[8,384,128]{2,1,0:T(8,128)(2,1)S(1)} %all-to-all-done.1.own_ref), channel_id=1, source_target_pairs={{0,1},{1,0},{2,3},{3,2},{4,5},{5,4},{6,7},{7,6},{8,9},{9,8},{10,11... | collective-permute-start | bytes 2359304 | tf_op jit(solution)/shard_map/ppermute | solution.py:276
  61.2 19.1 %collective-permute-start = (bf16[2,32,256]{2,1,0:T(8,128)(2,1)S(1)}, bf16[2,32,256]{2,1,0:T(8,128)(2,1)S(1)}, u32[]{:S(2)}, u32[]{:S(2)}) collective-permute-start(bf16[2,32,256]{2,1,0:T(8,128)(2,1)S(1)} %get-tuple-element.21), channel_id=1, source_target_pairs={{0,4},{4,8},{8,12},{12,16},{16,20},{20,24},{24,28},{28,32},{32,36}... | collective-permute-start | bytes 98312 | tf_op jit(solution)/shard_map/ppermute | solution.py:319
  64.3 21.2 %collective-permute-start.1 = (bf16[2,32,256]{2,1,0:T(8,128)(2,1)S(1)}, bf16[2,32,256]{2,1,0:T(8,128)(2,1)S(1)}, u32[]{:S(2)}, u32[]{:S(2)}) collective-permute-start(bf16[2,32,256]{2,1,0:T(8,128)(2,1)S(1)} %get-tuple-element.22), channel_id=1, source_target_pairs={{4,0},{8,4},{12,8},{16,12},{20,16},{24,20},{28,24},{32,28},{36,32}... | collective-permute-start | bytes 98312 | tf_op jit(solution)/shard_map/ppermute | solution.py:320
  87.0 6.0 %collective-permute-start.2 = (bf16[256,256]{1,0:T(8,128)(2,1)}, bf16[256,256]{1,0:T(8,128)(2,1)}, u32[]{:S(2)}, u32[]{:S(2)}) collective-permute-start(bf16[256,256]{1,0:T(8,128)(2,1)} %bitcast.9), channel_id=1, source_target_pairs={{0,2},{1,3},{2,0},{3,1},{4,6},{5,7},{6,4},{7,5},{8,10},{9,11},{10,... | collective-permute-start | bytes 393224 | tf_op jit(solution)/shard_map/ppermute | solution.py:276
  120.4 12.9 %copy-start = (f32[128,768]{1,0:T(8,128)S(1)}, f32[128,768]{1,0:T(8,128)}, u32[]{:S(2)}) copy-start(f32[128,768]{1,0:T(8,128)} %get-tuple-element.18.residual_ref) | copy-start | bytes 1179652
  120.4 9.8 %collective-permute-start.5 = (bf16[128,768]{1,0:T(8,128)(2,1)S(1)}, bf16[128,768]{1,0:T(8,128)(2,1)S(1)}, u32[]{:S(2)}, u32[]{:S(2)}) collective-permute-start(bf16[128,768]{1,0:T(8,128)(2,1)S(1)} %get-tuple-element.15), channel_id=1, source_target_pairs={{0,2},{1,3},{2,0},{3,1},{4,6},{5,7},{6,4},{7,5},{8,10},{9,11},{10,... | collective-permute-start | bytes 589832 | tf_op jit(solution)/shard_map/ppermute | solution.py:276
  123.8 9.5 %collective-permute-start.6 = (bf16[128,768]{1,0:T(8,128)(2,1)S(1)}, bf16[128,768]{1,0:T(8,128)(2,1)S(1)}, u32[]{:S(2)}, u32[]{:S(2)}) collective-permute-start(bf16[128,768]{1,0:T(8,128)(2,1)S(1)} %get-tuple-element.16), channel_id=1, source_target_pairs={{0,3},{1,2},{2,1},{3,0},{4,7},{5,6},{6,5},{7,4},{8,11},{9,10},{10,... | collective-permute-start | bytes 589832 | tf_op jit(solution)/shard_map/ppermute | solution.py:276
  127.7 5.6 %collective-permute-start.4 = (bf16[128,768]{1,0:T(8,128)(2,1)S(1)}, bf16[128,768]{1,0:T(8,128)(2,1)S(1)}, u32[]{:S(2)}, u32[]{:S(2)}) collective-permute-start(bf16[128,768]{1,0:T(8,128)(2,1)S(1)} %get-tuple-element.14), channel_id=1, source_target_pairs={{0,1},{1,0},{2,3},{3,2},{4,5},{5,4},{6,7},{7,6},{8,9},{9,8},{10,11... | collective-permute-start | bytes 589832 | tf_op jit(solution)/shard_map/ppermute | solution.py:276
